TPU v7x, 128 devices: a whole 4x4x4 slice. The times are simulated.
128 devices in a mesh: batch: 1, src: 16 (over z, y), graph: 8 (over x, core).
Axes of the slice: x: 4, y: 4, z: 4, core: 2. Of those that a mesh axis runs over, the one named last changes fastest.
Arguments:
- adj: bfloat16 [9216, 9216], P(('batch', 'graph'))
- sources: int32 [4096], P(('batch', 'src'))
- level_weight: float32 [2], replicated
Outputs:
- output: float32 [9216], P(('batch', 'graph'))
All inputs are finite; a program needn't handle non-finite values.
Results may differ from a plain program's by a relative error of at most 0.001.
Values are sent between devices in bfloat16 or wider.
A program may use at most 1 GiB of HBM per device.

v0:
```python
import functools

import jax
import jax.numpy as jnp
from jax import lax
from jax.experimental import pallas as pl
from jax.experimental.pallas import tpu as pltpu
from jax.sharding import PartitionSpec as P

MESH = pl.DeviceIdType.MESH
f32, bf16 = jnp.float32, jnp.bfloat16
CHUNKS = 2
TO_P, TO_Q = 0, 1


def rows_cols(lhs, rhs):
    return lax.dot_general(lhs, rhs, (((1,), (0,)), ((), ())), preferred_element_type=f32)


def rows_rows(lhs, rhs):
    return lax.dot_general(lhs, rhs, (((1,), (1,)), ((), ())), preferred_element_type=f32)


def kernel(ring, planes, scale, adj, src, lw, out,
           a_blk, a_oth, pick, ids, onehot, x1, x2own, x2rcv, part, wg,
           near0, far0, near, far, bc, total,
           load_sem, ssem, rsem, d2d_s, d2d_r, plane_s, plane_r):
    slab = a_oth.shape[0]
    cols_all = a_oth.shape[1]
    src_count = ids.shape[0]
    m = src_count // CHUNKS
    h = m // 2
    tile = 2 * slab // 3
    blk = min(32, h)

    g = lax.axis_index("graph")
    s_me = lax.axis_index("src")
    x, c = g // 2, g % 2
    odd = lax.rem(x, 2)
    chip_p = x + 1 - 2 * odd
    chip_q = lax.rem(x + ring - 1 + 2 * odd, ring)
    chip_far = lax.rem(x + 2, ring)
    to_p = {"graph": chip_p * 2 + c}
    to_q = {"graph": chip_q * 2 + c}
    to_mate = {"graph": x * 2 + (1 - c)}
    chips = (chip_far, chip_p, chip_q, x)
    slot = [pl.ds(i * slab, slab) for i in range(4)]
    FAR, NEAR_P, NEAR_Q, OWN = slot

    loads = {}
    for i, chip in enumerate(chips):
        for own in (0, 1):
            at = pl.ds(pl.multiple_of((chip * 2 + (c if own else 1 - c)) * slab, 128), slab)
            target = a_blk.at[pl.ds(0, slab), slot[i]] if own else a_oth.at[:, slot[i]]
            loads[own, i] = pltpu.make_async_copy(adj.at[:, at], target, load_sem.at[4 * own + i])
    for own, i in ((0, 0), (1, 0), (0, 1), (0, 2), (1, 1), (1, 2), (0, 3), (1, 3)):
        loads[own, i].start()

    barrier = pltpu.get_barrier_semaphore()
    for dev in (to_p, to_q, to_mate):
        pl.semaphore_signal(barrier, inc=1, device_id=dev, device_id_type=MESH)
    for o in range(1, planes):
        there = lax.rem(s_me + o, planes)
        pl.semaphore_signal(barrier, inc=1, device_id={"src": there}, device_id_type=MESH)
        pl.semaphore_signal(barrier, inc=1, device_id={"src": there, "graph": x * 2 + (1 - c)}, device_id_type=MESH)

    row = lax.broadcasted_iota(jnp.int32, (src_count, src_count), 0)
    col = lax.broadcasted_iota(jnp.int32, (src_count, src_count), 1)
    ids[...] = jnp.sum(jnp.where(row == col, src[...].astype(f32), 0.0), axis=1, keepdims=True)
    base = g * slab
    base_f = base.astype(f32)
    chip_f = (x * 2 * slab).astype(f32)
    lane = (lax.broadcasted_iota(jnp.int32, (blk, slab), 1) + base).astype(f32)

    def one_hot_rows(i, carry):
        r = pl.ds(pl.multiple_of(i * blk, blk), blk)
        onehot[r, :] = jnp.where(ids[r, :] == lane, 1.0, 0.0).astype(bf16)
        return carry

    lax.fori_loop(0, m // blk, one_hot_rows, 0)

    def mate_copy(i, source, target):
        return pltpu.make_async_remote_copy(src_ref=source, dst_ref=target, send_sem=d2d_s.at[i], recv_sem=d2d_r.at[i],
                                            device_id=to_mate, device_id_type=MESH)

    def ring_copy(stage, k, way, msg, source, target):
        i = ((stage * CHUNKS + k) * 2 + way) * 4 + msg
        return pltpu.make_async_remote_copy(src_ref=source, dst_ref=target, send_sem=ssem.at[i], recv_sem=rsem.at[i],
                                            device_id=to_p if way == TO_P else to_q, device_id_type=MESH)

    lo, hi = pl.ds(0, h), pl.ds(h, h)
    side = [pl.ds(0, slab), pl.ds(slab, slab)]
    own_half, mate_half = side
    merged = [pick.at[pl.ds(src_count + k * m, m), :] for k in range(CHUNKS)]
    two = [pl.ds(0, 2 * slab), pl.ds(2 * slab, 2 * slab)]

    def reduce_copies(stage, k):
        if stage == 0:
            send, nr, fr = merged[k], near0.at[k], far0.at[k]
        else:
            send, nr, fr = part.at[k], near.at[stage - 1, k], far.at[stage - 1, k]
        return {
            (TO_P, 0): ring_copy(stage, k, TO_P, 0, send.at[lo, FAR], fr.at[TO_P]),
            (TO_Q, 0): ring_copy(stage, k, TO_Q, 0, send.at[hi, FAR], fr.at[TO_Q]),
            (TO_P, 1): ring_copy(stage, k, TO_P, 1, send.at[lo, NEAR_P], nr.at[lo, side[TO_P]]),
            (TO_Q, 1): ring_copy(stage, k, TO_Q, 1, send.at[hi, NEAR_Q], nr.at[hi, side[TO_Q]]),
            (TO_P, 2): ring_copy(stage, k, TO_P, 2, send.at[hi, NEAR_P], nr.at[hi, side[TO_P]]),
            (TO_Q, 2): ring_copy(stage, k, TO_Q, 2, send.at[lo, NEAR_Q], nr.at[lo, side[TO_Q]]),
        }

    tail = slab // 256 * 128
    far_parts = [(2, 0, slab - tail), (3, slab - tail, tail)]

    def gather_copies(stage, k):
        buf = wg.at[k] if stage == 3 else part.at[k]
        if (stage, k) == (4, CHUNKS - 1):
            bands = far_parts
        else:
            bands = [(2, 0, slab)]
        relay = {}
        for msg, begin, width in bands:
            from_p, from_q, to_far = [pl.ds(n * slab + begin, width) for n in (1, 2, 0)]
            relay[TO_P, msg] = ring_copy(stage, k, TO_P, msg, buf.at[hi, from_q], buf.at[hi, to_far])
            relay[TO_Q, msg] = ring_copy(stage, k, TO_Q, msg, buf.at[lo, from_p], buf.at[lo, to_far])
        return {
            **relay,
            (TO_P, 0): ring_copy(stage, k, TO_P, 0, buf.at[lo, OWN], buf.at[lo, NEAR_P]),
            (TO_Q, 0): ring_copy(stage, k, TO_Q, 0, buf.at[hi, OWN], buf.at[hi, NEAR_Q]),
            (TO_P, 1): ring_copy(stage, k, TO_P, 1, buf.at[hi, OWN], buf.at[hi, NEAR_P]),
            (TO_Q, 1): ring_copy(stage, k, TO_Q, 1, buf.at[lo, OWN], buf.at[lo, NEAR_Q]),
        }

    copies = {}
    for k in range(CHUNKS):
        for stage in range(5):
            copies[stage, k] = reduce_copies(stage, k) if stage < 3 else gather_copies(stage, k)
    a_copies = [mate_copy(i, a_oth.at[:, slot[i]], a_blk.at[pl.ds(slab, slab), slot[i]]) for i in range(4)]
    m_copies = {(k, i): mate_copy(4 + 4 * k + i, pick.at[pl.ds(k * m, m), slot[i]], merged[k].at[:, slot[i]])
                for k in range(CHUNKS) for i in range(4)}
    first = 4 + 4 * CHUNKS
    x1_copies = [mate_copy(first + k, x1.at[k, :, own_half], x1.at[k, :, mate_half]) for k in range(CHUNKS)]
    x2_copies = [mate_copy(first + CHUNKS + k, x2own.at[k], x2rcv.at[k]) for k in range(CHUNKS)]
    z_copies = [mate_copy(first + 2 * CHUNKS + k, near.at[1, k, :, mate_half], near.at[0, k, :, mate_half]) for k in range(CHUNKS)]

    def by_rows(count, fn):
        def step(i, carry):
            fn(i)
            return carry
        lax.fori_loop(0, count // blk, step, 0)

    def rows_at(i, start=0):
        return pl.ds(pl.multiple_of(start + i * blk, blk), blk)

    def by_tiles(begin, end, fn):
        def step(t, carry):
            fn(pl.ds(pl.multiple_of(t * tile, 128), tile))
            return carry
        lax.fori_loop(begin, end, step, 0)

    def select_other(k, i):
        pick[pl.ds(k * m, m), slot[i]] = rows_cols(onehot[pl.ds(k * m, m), :], a_oth[:, slot[i]]).astype(bf16)

    def select_own(k, i):
        rk = pl.ds(k * m, m)
        here = (ids[rk, :] >= base_f) & (ids[rk, :] < base_f + slab)
        if (k, i) == (0, 0):
            x1[k, :, own_half] = rows_cols(onehot[rk, :], a_blk[pl.ds(0, slab), slot[i]]).astype(bf16)
            other(0, 1)
            m_copies[k, i].wait_recv()
            mine = x1[k, :, own_half].astype(f32)
        else:
            m_copies[k, i].wait_recv()
            mine = rows_cols(onehot[rk, :], a_blk[pl.ds(0, slab), slot[i]])
        merged[k][:, slot[i]] = jnp.where(here, mine, merged[k][:, slot[i]].astype(f32)).astype(bf16)

    def send_first(stage, k):
        cp = copies[stage, k]
        cp[TO_P, 0].start()
        cp[TO_Q, 0].start()
        cp[TO_P, 1].start()

    def start(stage, k):
        cp = copies[stage, k]
        if stage in (1, 2):
            for c_ in copies[stage - 1, k].values():
                c_.wait_send()

            def push(at):
                if stage == 1:
                    part[k, :, at] = rows_cols(x1[k], a_blk[:, at])
                else:
                    both = rows_cols(pick[pl.ds(0, 2 * m), two[0]], a_blk[:, at])
                    part[k, :, at] = both[:m] + both[m:]

            def mate_rows(pair):
                if (stage, k) == (1, 0):
                    for i in pair:
                        a_copies[i].wait_recv()

            mate_rows((0, 1))
            by_tiles(0, 3, push)
            send_first(stage, k)
            mate_rows((2, 3))
            by_tiles(3, 6, push)
            cp[TO_Q, 1].start()
        else:
            for msg in (0, 1):
                cp[TO_P, msg].start()
                cp[TO_Q, msg].start()

    def middle(stage, k):
        cp = copies[stage, k]
        for way in (TO_P, TO_Q):
            cp[way, 0].wait_recv()
            begin = 0 if way == TO_P else h
            dest = NEAR_Q if way == TO_P else NEAR_P
            if stage == 0:
                def select(i):
                    r = rows_at(i, begin)
                    rk = rows_at(i, k * m + begin)
                    here = (ids[rk, :] >= chip_f) & (ids[rk, :] < chip_f + 2 * slab)
                    merged[k][r, dest] = jnp.where(here, merged[k][r, dest].astype(f32),
                                                   far0[k, way, rows_at(i), :].astype(f32)).astype(bf16)
                by_rows(h, select)
            elif stage < 3:
                def add(i):
                    r = rows_at(i, begin)
                    part[k, r, dest] = part[k, r, dest] + far[stage - 1, k, way, rows_at(i), :]
                by_rows(h, add)
            cp[1 - way, 2].start()
            if (1 - way, 3) in cp:
                cp[1 - way, 3].start()

    def pull(buf, k, at, use, meanwhile=None):
        def split(i):
            r = rows_at(i)
            full = buf[k, r, at]
            top = full.astype(bf16)
            rest = full - top.astype(f32)
            mid = rest.astype(bf16)
            pick[r, at] = top
            pick[rows_at(i, m), at] = mid
            pick[rows_at(i, 2 * m), at] = (rest - mid.astype(f32)).astype(bf16)
        by_rows(m, split)

        def product(r):
            three = rows_rows(pick[pl.ds(0, 3 * m), at], a_blk[r, at])
            use(r, three[:m] + three[m:2 * m] + three[2 * m:])
        if meanwhile is None:
            by_tiles(0, 3, product)
        else:
            by_tiles(1, 3, product)
            meanwhile()
            by_tiles(0, 1, product)

    def close(k, at, z):
        bc[:, at] = bc[:, at] + jnp.sum(x1[k, :, at].astype(f32) * z, axis=0, keepdims=True)

    def last_far(n):
        k = CHUNKS - 1
        msg, begin, width = far_parts[n]
        copies[4, k][TO_P, msg].wait_recv()
        copies[4, k][TO_Q, msg].wait_recv()
        pull(part, k, pl.ds(begin, width), functools.partial(close, k))

    def last_own():
        pull(part, CHUNKS - 1, OWN, functools.partial(close, CHUNKS - 1))

    def last_nears():
        k = CHUNKS - 1
        copies[4, k][TO_P, 1].wait_recv()
        copies[4, k][TO_Q, 1].wait_recv()
        pull(part, k, pl.ds(slab, 2 * slab), functools.partial(close, k))

    def nears(stage, k):
        cp = copies[stage, k]
        cp[TO_P, 1].wait_recv()
        cp[TO_Q, 1].wait_recv()

        def keep(r, z):
            if stage == 3:
                near[1, k, :, r] = z
            else:
                close(k, r, z)
        pull(wg if stage == 3 else part, k, pl.ds(slab, 3 * slab), keep)

    def finish(stage, k):
        cp = copies[stage, k]
        for way in (TO_P, TO_Q):
            if stage < 3:
                cp[way, 1].wait_recv()
            cp[way, 2].wait_recv()
        if stage == 0:
            def first_level(i):
                r = rows_at(i)
                x1[k, r, own_half] = (merged[k][r, OWN].astype(f32) + near0[k, r, side[0]].astype(f32)
                                      + near0[k, r, side[1]].astype(f32)).astype(bf16)
            by_rows(m, first_level)
            x1_copies[k].start()
            if k == 0:
                a_copies[2].start()
                a_copies[3].start()
                for copy in m_copies.values():
                    copy.wait_send()
            x1_copies[k].wait_recv()
        elif stage == 1:
            def second_level(i):
                r = rows_at(i)
                rk = rows_at(i, k * m)
                total = part[k, r, OWN] + near[0, k, r, side[0]] + near[0, k, r, side[1]]
                seen = jnp.maximum(onehot[rk, :].astype(f32), x1[k, r, own_half].astype(f32))
                x2own[k, r, :] = total * (1.0 - seen)
            by_rows(m, second_level)
            x2_copies[k].start()

            def split(i, source, half):
                r = rows_at(i)
                full = source[k, r, :]
                top = full.astype(bf16)
                pick[r, half] = top
                pick[rows_at(i, m), half] = (full - top.astype(f32)).astype(bf16)
            by_rows(m, lambda i: split(i, x2own, own_half))
            x2_copies[k].wait_recv()
            by_rows(m, lambda i: split(i, x2rcv, mate_half))
        elif stage == 2:
            def third_level(i):
                r = rows_at(i)
                rk = rows_at(i, k * m)
                total = part[k, r, OWN] + near[1, k, r, side[0]] + near[1, k, r, side[1]]
                seen = jnp.maximum(onehot[rk, :].astype(f32), x1[k, r, own_half].astype(f32))
                seen = jnp.maximum(seen, jnp.where(x2own[k, r, :] > 0, 1.0, 0.0))
                paths = total * (1.0 - seen)
                reached = paths > 0
                wg[k, r, OWN] = jnp.where(reached, lw[1] / jnp.where(reached, paths, 1.0), 0.0)
            by_rows(m, third_level)
            for c_ in cp.values():
                c_.wait_send()
        elif stage == 3:
            def keep(r, z):
                near[1, k, :, r] = near[1, k, :, r] + z
            pull(wg, k, FAR, keep, z_copies[k].start)
            z_copies[k].wait_recv()

            def second_weights(i):
                r = rows_at(i)
                paths = x2own[k, r, :]
                delta = paths * (near[1, k, r, own_half] + near[0, k, r, mate_half])
                reached = paths > 0
                part[k, r, OWN] = jnp.where(reached, (lw[0] + delta) / jnp.where(reached, paths, 1.0), 0.0)
                bc[:, own_half] = bc[:, own_half] + jnp.sum(delta, axis=0, keepdims=True)
            by_rows(m, second_weights)
        else:
            pull(part, k, FAR, functools.partial(close, k))

    def other(k, i):
        if k == 0:
            loads[0, i].wait()
        select_other(k, i)
        if (k, i) == (0, 0):
            pl.semaphore_wait(barrier, 3 + 2 * (planes - 1))
        m_copies[k, i].start()

    def own(k, i):
        if k == 0:
            loads[1, i].wait()
        select_own(k, i)

    def first_level_sends(k):
        own(k, 0)
        copies[0, k][TO_P, 0].start()
        copies[0, k][TO_Q, 0].start()
        if k == 0:
            other(0, 2)
            a_copies[0].start()
        own(k, 1)
        copies[0, k][TO_P, 1].start()
        own(k, 2)
        copies[0, k][TO_Q, 1].start()

    other(0, 0)
    first_level_sends(0)
    lax.fori_loop(m // blk, src_count // blk, one_hot_rows, 0)
    bc[...] = jnp.zeros_like(bc)
    for i in range(3):
        other(1, i)
    a_copies[1].start()
    for k in range(CHUNKS):
        other(k, 3)
    middle(0, 0)
    first_level_sends(1)
    for k in range(CHUNKS):
        own(k, 3)
    middle(0, 1)
    for stage in range(1, 5):
        finish(stage - 1, 0)
        start(stage, 0)
        if stage == 4:
            nears(3, 1)
        middle(stage, 0)
        finish(stage - 1, 1)
        start(stage, 1)
        if stage >= 3:
            nears(stage, 0)
        if stage == 4:
            last_own()
        middle(stage, 1)
    finish(4, 0)
    last_nears()
    last_far(0)
    last_far(1)

    total[...] = bc[...] * scale
    keep_own = pltpu.make_async_copy(total.at[:, own_half], out.at[s_me], load_sem.at[0])
    keep_own.start()
    for o in range(planes):
        there = lax.rem(s_me + o, planes)
        for other_core in (0, 1):
            if o == 0 and not other_core:
                continue
            device = {"src": there, "graph": x * 2 + (1 - c)} if other_core else {"src": there}
            pltpu.make_async_remote_copy(src_ref=total.at[:, side[other_core]], dst_ref=out.at[other_core * planes + s_me],
                                         send_sem=plane_s, recv_sem=plane_r,
                                         device_id=device, device_id_type=MESH).start()

    for copy in a_copies + x1_copies + x2_copies + z_copies:
        copy.wait_send()
    for k in range(CHUNKS):
        for stage in (3, 4):
            for c_ in copies[stage, k].values():
                c_.wait_send()
    keep_own.wait()
    arrivals = out.at[pl.ds(0, 2 * planes - 1)]
    every = pltpu.make_async_remote_copy(src_ref=arrivals, dst_ref=arrivals, send_sem=plane_s, recv_sem=plane_r,
                                         device_id=to_mate, device_id_type=MESH)
    every.wait_recv()
    every.wait_send()


def solution(mesh):
    planes = mesh.shape["src"]
    ring = mesh.shape["graph"] // 2

    def device_program(adj_slab, src_local, level_weight):
        slab, vertex_count = adj_slab.shape
        src_count = src_local.shape[0]
        m = src_count // CHUNKS
        scale = vertex_count / (src_count * planes * (level_weight.shape[0] + 1) ** 3)
        wide = 4 * slab
        vmem = pltpu.VMEM
        sem = pltpu.SemaphoreType.DMA
        mates = 4 + 7 * CHUNKS
        rings = 5 * CHUNKS * 8
        flops = 2 * 9 * src_count * slab * vertex_count
        bc = pl.pallas_call(
            functools.partial(kernel, ring, planes, scale),
            out_shape=jax.ShapeDtypeStruct((2 * planes, 1, slab), f32),
            in_specs=[pl.BlockSpec(memory_space=pl.ANY), pl.BlockSpec(memory_space=vmem), pl.BlockSpec(memory_space=pltpu.SMEM)],
            out_specs=pl.BlockSpec(memory_space=pl.ANY),
            scratch_shapes=[
                vmem((2 * slab, wide), bf16), vmem((slab, wide), bf16),
                vmem((2 * src_count, wide), bf16), vmem((src_count, 1), f32), vmem((src_count, slab), bf16),
                vmem((CHUNKS, m, 2 * slab), bf16), vmem((CHUNKS, m, slab), f32), vmem((CHUNKS, m, slab), f32),
                vmem((CHUNKS, m, wide), f32), vmem((CHUNKS, m, wide), f32),
                vmem((CHUNKS, m, 2 * slab), bf16), vmem((CHUNKS, 2, m // 2, slab), bf16),
                vmem((2, CHUNKS, m, 2 * slab), f32), vmem((2, CHUNKS, 2, m // 2, slab), f32),
                vmem((1, 2 * slab), f32), vmem((1, 2 * slab), f32),
                sem((8,)), sem((rings,)), sem((rings,)), sem((mates,)), sem((mates,)), sem, sem,
            ],
            compiler_params=pltpu.CompilerParams(collective_id=0, has_side_effects=True, vmem_limit_bytes=67043328),
            cost_estimate=pl.CostEstimate(flops=flops, bytes_accessed=2 * slab * vertex_count, transcendentals=0),
        )(adj_slab, src_local.reshape(1, src_count), level_weight)
        return jnp.sum(bc, axis=(0, 1))

    return jax.shard_map(device_program, mesh=mesh,
                         in_specs=(P(("batch", "graph"), None), P(("batch", "src")), P(None)),
                         out_specs=P(("batch", "graph")), check_vma=False)
```

profile of v0, /device:TPU:1, one launch (start us, length us, event | category | flops | bytes accessed | tf_op | source)
XLA Modules:
  0.0 195.5 jit_solution(7162037808168547454)
XLA Ops:
  0.0 193.9 %shard_map.37 = f32[32,1,1152]{2,1,0:T(1,128)} custom-call(bf16[1152,9216]{1,0:T(8,128)(2,1)} %adj.1, s32[1,256]{1,0:T(1,128)} %bitcast.1, f32[2]{0:T(128)} %lw.1), custom_call_target="tpu_custom_call" | custom-call | flops 48922361856 | bytes 21233664 | tf_op jit(solution)/shard_map/pallas_call | solution.py:454
  193.9 1.6 reduce_sum.9
where the time goes:
time: 196 us; the launch traced here: 195 us
  Pallas kernels  194 us (99%)
    pallas_call x1, Pallas kernels, device_program(): pl.pallas_call(functools.partial(kernel, ring, planes, scale), out_shape=...  194 us

commit v1 on v0

--- a/solution.py
+++ b/solution.py
@@ -53,8 +53,9 @@
             at = pl.ds(pl.multiple_of((chip * 2 + (c if own else 1 - c)) * slab, 128), slab)
             target = a_blk.at[pl.ds(0, slab), slot[i]] if own else a_oth.at[:, slot[i]]
             loads[own, i] = pltpu.make_async_copy(adj.at[:, at], target, load_sem.at[4 * own + i])
-    for own, i in ((0, 0), (1, 0), (0, 1), (0, 2), (1, 1), (1, 2), (0, 3), (1, 3)):
-        loads[own, i].start()
+    load_order = ((0, 0), (1, 0), (0, 1), (0, 2), (1, 1), (1, 2), (0, 3), (1, 3))
+    for at in load_order[:2]:
+        loads[at].start()
 
     barrier = pltpu.get_barrier_semaphore()
     for dev in (to_p, to_q, to_mate):
@@ -298,7 +299,6 @@
             by_rows(m, first_level)
             x1_copies[k].start()
             if k == 0:
-                a_copies[2].start()
                 a_copies[3].start()
                 for copy in m_copies.values():
                     copy.wait_send()
@@ -355,6 +355,9 @@
     def other(k, i):
         if k == 0:
             loads[0, i].wait()
+        if (k, i) == (0, 0):
+            for at in load_order[2:]:
+                loads[at].start()
         select_other(k, i)
         if (k, i) == (0, 0):
             pl.semaphore_wait(barrier, 3 + 2 * (planes - 1))
@@ -386,6 +389,7 @@
     a_copies[1].start()
     for k in range(CHUNKS):
         other(k, 3)
+    a_copies[2].start()
     middle(0, 0)
     first_level_sends(1)
     for k in range(CHUNKS):

time: 196 us -> 195 us (level)
  no operation moved by 1% of the time
where the time goes in v1:
time: 195 us
  Pallas kernels  194 us (99%)
    pallas_call x1, Pallas kernels, device_program(): pl.pallas_call(functools.partial(kernel, ring, planes, scale), out_shape=...  194 us

profile of v1, /device:TPU:1, one launch (start us, length us, event | category | flops | bytes accessed | tf_op | source)
XLA Modules:
  0.0 195.4 jit_solution(14757084662370851319)
XLA Ops:
  0.0 193.7 %shard_map.37 = f32[32,1,1152]{2,1,0:T(1,128)} custom-call(bf16[1152,9216]{1,0:T(8,128)(2,1)} %adj.1, s32[1,256]{1,0:T(1,128)} %bitcast.1, f32[2]{0:T(128)} %lw.1), custom_call_target="tpu_custom_call" | custom-call | flops 48922361856 | bytes 21233664 | tf_op jit(solution)/shard_map/pallas_call | solution.py:458
  193.7 1.6 reduce_sum.9

commit v2 on v1

--- a/solution.py
+++ b/solution.py
@@ -58,12 +58,13 @@
         loads[at].start()
 
     barrier = pltpu.get_barrier_semaphore()
-    for dev in (to_p, to_q, to_mate):
-        pl.semaphore_signal(barrier, inc=1, device_id=dev, device_id_type=MESH)
-    for o in range(1, planes):
+    for o in sorted(range(1, planes), key=lambda o: abs(o - planes // 2)):
         there = lax.rem(s_me + o, planes)
         pl.semaphore_signal(barrier, inc=1, device_id={"src": there}, device_id_type=MESH)
         pl.semaphore_signal(barrier, inc=1, device_id={"src": there, "graph": x * 2 + (1 - c)}, device_id_type=MESH)
+
+    for dev in (to_p, to_q, to_mate):
+        pl.semaphore_signal(barrier, inc=1, device_id=dev, device_id_type=MESH)
 
     row = lax.broadcasted_iota(jnp.int32, (src_count, src_count), 0)
     col = lax.broadcasted_iota(jnp.int32, (src_count, src_count), 1)

time: 195 us -> 195 us (level)
  no operation moved by 1% of the time
where the time goes in v2:
time: 195 us
  Pallas kernels  194 us (99%)
    pallas_call x1, Pallas kernels, device_program(): pl.pallas_call(functools.partial(kernel, ring, planes, scale), out_shape=...  194 us

profile of v2, /device:TPU:1, one launch (start us, length us, event | category | flops | bytes accessed | tf_op | source)
XLA Modules:
  0.0 195.4 jit_solution(3606012096362092853)
XLA Ops:
  0.0 193.7 %shard_map.37 = f32[32,1,1152]{2,1,0:T(1,128)} custom-call(bf16[1152,9216]{1,0:T(8,128)(2,1)} %adj.1, s32[1,256]{1,0:T(1,128)} %bitcast.1, f32[2]{0:T(128)} %lw.1), custom_call_target="tpu_custom_call" | custom-call | flops 48922361856 | bytes 21233664 | tf_op jit(solution)/shard_map/pallas_call | solution.py:459
  193.7 1.6 reduce_sum.9

commit v3 on v0

--- a/solution.py
+++ b/solution.py
@@ -10,6 +10,7 @@
 MESH = pl.DeviceIdType.MESH
 f32, bf16 = jnp.float32, jnp.bfloat16
 CHUNKS = 2
+SIDE = 4
 TO_P, TO_Q = 0, 1
 
 
@@ -24,7 +25,7 @@
 def kernel(ring, planes, scale, adj, src, lw, out,
            a_blk, a_oth, pick, ids, onehot, x1, x2own, x2rcv, part, wg,
            near0, far0, near, far, bc, total,
-           load_sem, ssem, rsem, d2d_s, d2d_r, plane_s, plane_r):
+           load_sem, ssem, rsem, d2d_s, d2d_r, plane_s, plane_r, rounds):
     slab = a_oth.shape[0]
     cols_all = a_oth.shape[1]
     src_count = ids.shape[0]
@@ -59,10 +60,21 @@
     barrier = pltpu.get_barrier_semaphore()
     for dev in (to_p, to_q, to_mate):
         pl.semaphore_signal(barrier, inc=1, device_id=dev, device_id_type=MESH)
-    for o in range(1, planes):
-        there = lax.rem(s_me + o, planes)
-        pl.semaphore_signal(barrier, inc=1, device_id={"src": there}, device_id_type=MESH)
-        pl.semaphore_signal(barrier, inc=1, device_id={"src": there, "graph": x * 2 + (1 - c)}, device_id_type=MESH)
+    if planes == SIDE * SIDE:
+        row_, col_ = s_me // SIDE, lax.rem(s_me, SIDE)
+        around = [{"src": row_ * SIDE + lax.rem(col_ + step, SIDE)} for step in (1, SIDE - 1)]
+        around += [{"src": lax.rem(row_ + step, SIDE) * SIDE + col_} for step in (1, SIDE - 1)]
+    else:
+        around = [{"src": lax.rem(s_me + o, planes), "graph": x * 2 + core} for o in range(1, planes) for core in (0, 1)]
+    for dev in around:
+        pl.semaphore_signal(barrier, inc=1, device_id=dev, device_id_type=MESH)
+
+    def tell(n):
+        for dev in around:
+            pl.semaphore_signal(rounds.at[n], inc=1, device_id=dev, device_id_type=MESH)
+
+    def hear(n):
+        pl.semaphore_wait(rounds.at[n], len(around))
 
     row = lax.broadcasted_iota(jnp.int32, (src_count, src_count), 0)
     col = lax.broadcasted_iota(jnp.int32, (src_count, src_count), 1)
@@ -298,7 +310,6 @@
             by_rows(m, first_level)
             x1_copies[k].start()
             if k == 0:
-                a_copies[2].start()
                 a_copies[3].start()
                 for copy in m_copies.values():
                     copy.wait_send()
@@ -357,7 +368,8 @@
             loads[0, i].wait()
         select_other(k, i)
         if (k, i) == (0, 0):
-            pl.semaphore_wait(barrier, 3 + 2 * (planes - 1))
+            pl.semaphore_wait(barrier, 3 + len(around))
+            tell(0)
         m_copies[k, i].start()
 
     def own(k, i):
@@ -386,6 +398,7 @@
     a_copies[1].start()
     for k in range(CHUNKS):
         other(k, 3)
+    a_copies[2].start()
     middle(0, 0)
     first_level_sends(1)
     for k in range(CHUNKS):
@@ -397,6 +410,9 @@
         if stage == 4:
             nears(3, 1)
         middle(stage, 0)
+        hear(stage - 1)
+        if stage < 4:
+            tell(stage)
         finish(stage - 1, 1)
         start(stage, 1)
         if stage >= 3:
@@ -464,7 +480,7 @@
                 vmem((CHUNKS, m, 2 * slab), bf16), vmem((CHUNKS, 2, m // 2, slab), bf16),
                 vmem((2, CHUNKS, m, 2 * slab), f32), vmem((2, CHUNKS, 2, m // 2, slab), f32),
                 vmem((1, 2 * slab), f32), vmem((1, 2 * slab), f32),
-                sem((8,)), sem((rings,)), sem((rings,)), sem((mates,)), sem((mates,)), sem, sem,
+                sem((8,)), sem((rings,)), sem((rings,)), sem((mates,)), sem((mates,)), sem, sem, pltpu.SemaphoreType.REGULAR((4,)),
             ],
             compiler_params=pltpu.CompilerParams(collective_id=0, has_side_effects=True, vmem_limit_bytes=67043328),
             cost_estimate=pl.CostEstimate(flops=flops, bytes_accessed=2 * slab * vertex_count, transcendentals=0),

time: 196 us -> 195 us (level)
  no operation moved by 1% of the time
where the time goes in v3:
time: 195 us
  Pallas kernels  193 us (99%)
    pallas_call x1, Pallas kernels, device_program(): pl.pallas_call(functools.partial(kernel, ring, planes, scale), out_shape=...  193 us

profile of v3, /device:TPU:1, one launch (start us, length us, event | category | flops | bytes accessed | tf_op | source)
XLA Modules:
  0.0 194.9 jit_solution(15864141431403988403)
XLA Ops:
  0.0 193.3 %shard_map.37 = f32[32,1,1152]{2,1,0:T(1,128)} custom-call(bf16[1152,9216]{1,0:T(8,128)(2,1)} %adj.1, s32[1,256]{1,0:T(1,128)} %bitcast.1, f32[2]{0:T(128)} %lw.1), custom_call_target="tpu_custom_call" | custom-call | flops 48922361856 | bytes 21233664 | tf_op jit(solution)/shard_map/pallas_call | solution.py:470
  193.3 1.6 reduce_sum.9

commit v4 on v3

--- a/solution.py
+++ b/solution.py
@@ -428,7 +428,10 @@
     total[...] = bc[...] * scale
     keep_own = pltpu.make_async_copy(total.at[:, own_half], out.at[s_me], load_sem.at[0])
     keep_own.start()
-    for o in range(planes):
+    def distance(o):
+        return -sum(min(n, SIDE - n) for n in (o % SIDE, o // SIDE))
+
+    for o in sorted(range(planes), key=distance):
         there = lax.rem(s_me + o, planes)
         for other_core in (0, 1):
             if o == 0 and not other_core:

time: 195 us -> 195 us (level)
  no operation moved by 1% of the time
where the time goes in v4:
time: 195 us
  Pallas kernels  194 us (99%)
    pallas_call x1, Pallas kernels, device_program(): pl.pallas_call(functools.partial(kernel, ring, planes, scale), out_shape=...  194 us

profile of v4, /device:TPU:1, one launch (start us, length us, event | category | flops | bytes accessed | tf_op | source)
XLA Modules:
  0.0 195.3 jit_solution(8274017889679086214)
XLA Ops:
  0.0 193.7 %shard_map.37 = f32[32,1,1152]{2,1,0:T(1,128)} custom-call(bf16[1152,9216]{1,0:T(8,128)(2,1)} %adj.1, s32[1,256]{1,0:T(1,128)} %bitcast.1, f32[2]{0:T(128)} %lw.1), custom_call_target="tpu_custom_call" | custom-call | flops 48922361856 | bytes 21233664 | tf_op jit(solution)/shard_map/pallas_call | solution.py:473
  193.7 1.6 reduce_sum.9

commit v5 on v3

--- a/solution.py
+++ b/solution.py
@@ -163,11 +163,11 @@
     def rows_at(i, start=0):
         return pl.ds(pl.multiple_of(start + i * blk, blk), blk)
 
-    def by_tiles(begin, end, fn):
+    def by_tiles(begin, end, fn, unroll=False):
         def step(t, carry):
             fn(pl.ds(pl.multiple_of(t * tile, 128), tile))
             return carry
-        lax.fori_loop(begin, end, step, 0)
+        lax.fori_loop(begin, end, step, 0, unroll=unroll)
 
     def select_other(k, i):
         pick[pl.ds(k * m, m), slot[i]] = rows_cols(onehot[pl.ds(k * m, m), :], a_oth[:, slot[i]]).astype(bf16)
@@ -243,7 +243,7 @@
             if (1 - way, 3) in cp:
                 cp[1 - way, 3].start()
 
-    def pull(buf, k, at, use, meanwhile=None):
+    def pull(buf, k, at, use, meanwhile=None, unroll=False):
         def split(i):
             r = rows_at(i)
             full = buf[k, r, at]
@@ -259,7 +259,7 @@
             three = rows_rows(pick[pl.ds(0, 3 * m), at], a_blk[r, at])
             use(r, three[:m] + three[m:2 * m] + three[2 * m:])
         if meanwhile is None:
-            by_tiles(0, 3, product)
+            by_tiles(0, 3, product, unroll)
         else:
             by_tiles(1, 3, product)
             meanwhile()
@@ -273,7 +273,7 @@
         msg, begin, width = far_parts[n]
         copies[4, k][TO_P, msg].wait_recv()
         copies[4, k][TO_Q, msg].wait_recv()
-        pull(part, k, pl.ds(begin, width), functools.partial(close, k))
+        pull(part, k, pl.ds(begin, width), functools.partial(close, k), unroll=True)
 
     def last_own():
         pull(part, CHUNKS - 1, OWN, functools.partial(close, CHUNKS - 1))

time: 195 us -> 195 us (level)
  no operation moved by 1% of the time
where the time goes in v5:
time: 195 us
  Pallas kernels  193 us (99%)
    pallas_call x1, Pallas kernels, device_program(): pl.pallas_call(functools.partial(kernel, ring, planes, scale), out_shape=...  193 us

profile of v5, /device:TPU:1, one launch (start us, length us, event | category | flops | bytes accessed | tf_op | source)
XLA Modules:
  0.0 194.6 jit_solution(5565965381406318208)
XLA Ops:
  0.0 192.9 %shard_map.37 = f32[32,1,1152]{2,1,0:T(1,128)} custom-call(bf16[1152,9216]{1,0:T(8,128)(2,1)} %adj.1, s32[1,256]{1,0:T(1,128)} %bitcast.1, f32[2]{0:T(128)} %lw.1), custom_call_target="tpu_custom_call" | custom-call | flops 48922361856 | bytes 21233664 | tf_op jit(solution)/shard_map/pallas_call | solution.py:470
  193.0 1.6 reduce_sum.9
